TPU v7x, 256 devices: a whole 4x4x8 slice. The times are simulated.
256 devices in a mesh: ta: 16 (over z, core), gy: 2 (over x_lo), gx: 8 (over x_hi, y).
Axes of the slice: x: 4 (x_hi: 2, x_lo: 2; x = x_hi * 2 + x_lo), y: 4, z: 8, core: 2. Of those that a mesh axis runs over, the one named last changes fastest.
Arguments:
- queries: bfloat16 [16, 2, 16, 64, 1536], P('ta', 'gy', 'gx'), may hold values from -24 to 24
- keys: bfloat16 [16, 2, 16, 64, 1536], P('ta', 'gy', 'gx'), may hold values from -24 to 24
- values: bfloat16 [16, 2, 16, 64, 1536], P('ta', 'gy', 'gx'), may hold values from -6 to 6
- grad_out: bfloat16 [16, 2, 16, 64, 1536], P('ta', 'gy', 'gx'), may hold values from -6 to 6
Outputs:
- attention: bfloat16 [16, 2, 16, 64, 1536], P('ta', 'gy', 'gx')
- grad_queries: bfloat16 [16, 2, 16, 64, 1536], P('ta', 'gy', 'gx')
- grad_keys: bfloat16 [16, 2, 16, 64, 1536], P('ta', 'gy', 'gx')
- grad_values: bfloat16 [16, 2, 16, 64, 1536], P('ta', 'gy', 'gx')
All inputs are finite; a program needn't handle non-finite values.
Results may differ from a plain program's by a relative error of at most 0.019.
Values may be sent and summed in bfloat16 or wider, within the bound.
A program may use at most 128 MiB of HBM per device.

v0:
```python
import jax
import jax.numpy as jnp
from jax import lax
from jax.experimental import pallas as pl
from jax.experimental.pallas import tpu as pltpu
from jax.sharding import PartitionSpec as P

MESH = pl.DeviceIdType.MESH
DIM = 128
TOK = 64
CHUNKS = 3
FACTOR = DIM ** -0.5
SCALE = FACTOR * 1.4426950408889634
FAR = 1e30
FRAMES = 16
TCOLS = 16
NT = (((1,), (1,)), ((), ()))
NN = (((1,), (0,)), ((), ()))


def dot_nt(a, b):
    return lax.dot_general(a, b, NT, preferred_element_type=jnp.float32)


def dot_nn(a, b):
    return lax.dot_general(a, b, NN, preferred_element_type=jnp.float32)


def kernel(
    q_in, k_in, v_in, g_in, out_o, out_dq, out_dk, out_dv,
    kv, qg, st, stage,
    local_sem, in_send, in_recv, y_send, y_recv, z_send, z_recv,
    sy_send, sy_recv, sz_send, sz_recv, keep_sem, back_send, back_recv,
):
    ta = lax.axis_index("ta")
    xl = lax.axis_index("gy")
    gx = lax.axis_index("gx")
    z, core = ta // 2, ta % 2
    xh = gx // 4
    side = (xl + xh) % 2

    def along_y(step):
        other = (gx + step + 8) % 8
        return (ta, (side + other // 4) % 2, other)

    def along_z(step):
        return (((z + step + 8) % 8) * 2 + core, xl, gx)

    peers = ((0, 1), (1, 0), (1, 1))

    def peer_id(p):
        dx, dc = peers[p]
        return (z * 2 + (core + dc) % 2, (xl + dx) % 2, gx)

    def peer_group(p):
        dx, dc = peers[p]
        return 2 * ((side + dx) % 2) + (core + dc) % 2

    my_group = 2 * side + core
    y_ids = (along_y(1), along_y(-1))
    z_ids = (along_z(1), along_z(-1))

    barrier = pltpu.get_barrier_semaphore()
    for target in (peer_id(0), peer_id(1), peer_id(2), *y_ids, *z_ids):
        pl.semaphore_signal(barrier, inc=1, device_id=target, device_id_type=MESH)
    pl.semaphore_wait(barrier, 7)

    def lanes(group, j):
        return pl.ds(pl.multiple_of((group * CHUNKS + j) * DIM, DIM), DIM)

    sources = (k_in, v_in, q_in, g_in)
    results = (out_o, out_dq, out_dk, out_dv)

    def slot(t, j):
        held = kv if t < 2 else qg
        return held.at[j, t % 2, pl.ds(1, 2), 1 + core, xl]

    def local_copy(j, t):
        return pltpu.make_async_copy(
            sources[t].at[0, 0, :, :, lanes(my_group, j)], slot(t, j), local_sem.at[j, t]
        )

    def in_copy(p, j, t):
        return pltpu.make_async_remote_copy(
            src_ref=sources[t].at[0, 0, :, :, lanes(peer_group(p), j)],
            dst_ref=slot(t, j),
            send_sem=in_send.at[p, j, t],
            recv_sem=in_recv.at[p, j, t],
            device_id=peer_id(p),
            device_id_type=MESH,
        )

    def remote(src, dst, send, recv, target):
        return pltpu.make_async_remote_copy(
            src_ref=src, dst_ref=dst, send_sem=send, recv_sem=recv,
            device_id=target, device_id_type=MESH,
        )

    def kv_y(j, w, d):
        row = (xl + w) % 2
        return remote(
            kv.at[j, :, 2 - d, pl.ds(1, 2), row], kv.at[j, :, 3 * d, pl.ds(1, 2), row],
            y_send.at[0, j, w, d], y_recv.at[0, j, row, d], y_ids[d],
        )

    def qg_z(j, w, d):
        row = (xl + w) % 2
        return remote(
            qg.at[j, :, pl.ds(1, 2), 2 - d, row], qg.at[j, :, pl.ds(1, 2), 3 * d, row],
            z_send.at[0, j, w, d], z_recv.at[0, j, row, d], z_ids[d],
        )

    def kv_z(j, d):
        return remote(
            kv.at[j, :, :, 2 - d], kv.at[j, :, :, 3 * d],
            z_send.at[1, j, 0, d], z_recv.at[1, j, 0, d], z_ids[d],
        )

    def qg_y(j, d):
        return remote(
            qg.at[j, :, 2 - d], qg.at[j, :, 3 * d],
            y_send.at[1, j, 0, d], y_recv.at[1, j, 0, d], y_ids[d],
        )

    def st_y(j, d):
        return remote(
            st.at[j, 2 - d, pl.ds(1, 2)], st.at[j, 3 * d, pl.ds(1, 2)],
            sy_send.at[j, d], sy_recv.at[j, d], y_ids[d],
        )

    def st_z(j, d):
        return remote(
            st.at[j, :, 2 - d], st.at[j, :, 3 * d],
            sz_send.at[j, d], sz_recv.at[j, d], z_ids[d],
        )

    def keep_copy(t, j):
        return pltpu.make_async_copy(
            stage.at[t, j, :, core, xl], results[t].at[0, 0, :, :, lanes(my_group, j)],
            keep_sem.at[t, j],
        )

    def back_copy(p, t, j):
        dx, dc = peers[p]
        return remote(
            stage.at[t, j, :, (core + dc) % 2, (xl + dx) % 2],
            results[t].at[0, 0, :, :, lanes(my_group, j)],
            back_send.at[p, t, j], back_recv.at[p, t, j], peer_id(p),
        )

    for j in range(CHUNKS):
        for t in range(4):
            local_copy(j, t).start()
            in_copy(0, j, t).start()
    for j in range(CHUNKS):
        for t in range(4):
            for p in (1, 2):
                in_copy(p, j, t).start()

    def first_hops(j, w):
        for half in range(2):
            for t in (2 * half, 2 * half + 1):
                if w == 0:
                    local_copy(j, t).wait()
                    in_copy(0, j, t).wait_recv()
                else:
                    in_copy(1, j, t).wait_recv()
                    in_copy(2, j, t).wait_recv()
            for d in range(2):
                (kv_y if half == 0 else qg_z)(j, w, d).start()

    def second_hops(j):
        for d in range(2):
            kv_y(j, 0, d).wait_recv()
            kv_y(j, 1, d).wait_recv()
        for d in range(2):
            kv_z(j, d).start()
        for d in range(2):
            qg_z(j, 0, d).wait_recv()
            qg_z(j, 1, d).wait_recv()
        for d in range(2):
            qg_y(j, d).start()

    def in_grid(c, f, dc, df):
        col = 2 * gx + c + dc - 1
        frame = 2 * z + f + df - 1
        return (col >= 0) & (col < TCOLS) & (frame >= 0) & (frame < FRAMES)

    lane = lax.broadcasted_iota(jnp.int32, (DIM, DIM), 1)

    def query_block(j, c, f):
        q = qg[j, 0, 1 + c, 1 + f].reshape(2 * TOK, DIM)
        g = qg[j, 1, 1 + c, 1 + f].reshape(2 * TOK, DIM)
        scores = []
        for dc in range(3):
            s = dot_nt(q, kv[j, 0, c + dc, pl.ds(f, 3)].reshape(6 * TOK, DIM))
            parts = [
                s[:, df * DIM:(df + 1) * DIM] * SCALE
                + jnp.where(in_grid(c, f, dc, df), 0.0, -FAR)
                for df in range(3)
            ]
            scores.append(jnp.concatenate(parts, axis=1))
        top = jnp.maximum(jnp.maximum(scores[0], scores[1]), scores[2])
        top = jnp.max(top, axis=1, keepdims=True)
        powers = [jnp.exp2(s - top) for s in scores]
        total = jnp.sum(powers[0] + powers[1] + powers[2], axis=1, keepdims=True)
        scale = 1.0 / total
        att = jnp.zeros((2 * TOK, DIM), jnp.float32)
        for dc in range(3):
            v = kv[j, 1, c + dc, pl.ds(f, 3)].reshape(6 * TOK, DIM)
            att += dot_nn(powers[dc].astype(jnp.bfloat16), v)
        att = (att * scale).astype(jnp.bfloat16)
        dots = jnp.sum(g.astype(jnp.float32) * att.astype(jnp.float32), axis=1, keepdims=True)
        grad = jnp.zeros((2 * TOK, DIM), jnp.float32)
        for dc in range(3):
            k = kv[j, 0, c + dc, pl.ds(f, 3)].reshape(6 * TOK, DIM)
            v = kv[j, 1, c + dc, pl.ds(f, 3)].reshape(6 * TOK, DIM)
            slopes = powers[dc] * (dot_nt(g, v) - dots)
            grad += dot_nn(slopes.astype(jnp.bfloat16), k)
        grad = (grad * (scale * FACTOR)).astype(jnp.bfloat16)
        stage[0, j, c, f] = att.reshape(2, TOK, DIM)
        stage[1, j, c, f] = grad.reshape(2, TOK, DIM)
        both = jnp.where(lane == 0, top + jnp.log2(total), dots)
        st[j, 1 + c, 1 + f] = jnp.transpose(both)[:8]

    def key_block(j, c, f):
        k = kv[j, 0, 1 + c, 1 + f].reshape(2 * TOK, DIM)
        v = kv[j, 1, 1 + c, 1 + f].reshape(2 * TOK, DIM)
        grad_k = jnp.zeros((2 * TOK, DIM), jnp.float32)
        grad_v = jnp.zeros((2 * TOK, DIM), jnp.float32)
        for dc in range(3):
            q = qg[j, 0, c + dc, pl.ds(f, 3)].reshape(6 * TOK, DIM)
            g = qg[j, 1, c + dc, pl.ds(f, 3)].reshape(6 * TOK, DIM)
            s = dot_nt(k, q)
            pulls = dot_nt(v, g)
            weights, slopes = [], []
            for df in range(3):
                tile = st[j, c + dc, f + df]
                level = jnp.where(in_grid(c, f, dc, df), tile[0:1], FAR)
                cut = slice(df * DIM, (df + 1) * DIM)
                w = jnp.exp2(s[:, cut] * SCALE - level)
                weights.append(w.astype(jnp.bfloat16))
                slopes.append((w * (pulls[:, cut] - tile[1:2])).astype(jnp.bfloat16))
            grad_v += dot_nn(jnp.concatenate(weights, axis=1), g)
            grad_k += dot_nn(jnp.concatenate(slopes, axis=1), q)
        stage[2, j, c, f] = (grad_k * FACTOR).astype(jnp.bfloat16).reshape(2, TOK, DIM)
        stage[3, j, c, f] = grad_v.astype(jnp.bfloat16).reshape(2, TOK, DIM)

    def blocks(run, j, first, last):
        def one(i, carry):
            run(j, i // 2, i % 2)
            return carry

        lax.fori_loop(first, last, one, 0)

    def send_back(j, ts):
        for t in ts:
            for p in (1, 2, 0):
                back_copy(p, t, j).start()
            keep_copy(t, j).start()

    def query_side(j):
        for d in range(2):
            kv_z(j, d).wait_recv()
        blocks(query_block, j, 0, 4)
        for d in range(2):
            st_y(j, d).start()
        send_back(j, (0, 1))

    def pass_stats(j):
        for d in range(2):
            st_y(j, d).wait_recv()
        for d in range(2):
            st_z(j, d).start()

    def key_ready(j):
        for d in range(2):
            qg_y(j, d).wait_recv()
        for d in range(2):
            st_z(j, d).wait_recv()

    for j in range(CHUNKS):
        first_hops(j, 0)
    first_hops(0, 1)
    second_hops(0)
    first_hops(1, 1)
    second_hops(1)
    first_hops(2, 1)
    query_side(0)
    second_hops(2)
    pass_stats(0)
    query_side(1)
    key_ready(0)
    blocks(key_block, 0, 0, 4)
    send_back(0, (2, 3))
    pass_stats(1)
    query_side(2)
    key_ready(1)
    blocks(key_block, 1, 0, 2)
    pass_stats(2)
    blocks(key_block, 1, 2, 4)
    send_back(1, (2, 3))
    key_ready(2)
    blocks(key_block, 2, 0, 4)
    send_back(2, (2, 3))

    for j in range(CHUNKS):
        for t in range(4):
            for p in range(3):
                in_copy(p, j, t).wait_send()
        for d in range(2):
            for w in range(2):
                kv_y(j, w, d).wait_send()
                qg_z(j, w, d).wait_send()
            kv_z(j, d).wait_send()
            qg_y(j, d).wait_send()
            st_y(j, d).wait_send()
            st_z(j, d).wait_send()
        for t in range(4):
            keep_copy(t, j).wait()
            for p in range(3):
                back_copy(p, t, j).wait_send()
                back_copy(p, t, j).wait_recv()


def body(queries, keys, values, grad_out):
    dma = pltpu.SemaphoreType.DMA
    block = (CHUNKS, 2, 4, 4, 2, TOK, DIM)
    return pl.pallas_call(
        kernel,
        out_shape=[jax.ShapeDtypeStruct(queries.shape, jnp.bfloat16)] * 4,
        in_specs=[pl.BlockSpec(memory_space=pl.ANY)] * 4,
        out_specs=[pl.BlockSpec(memory_space=pl.ANY)] * 4,
        scratch_shapes=[
            pltpu.VMEM(block, jnp.bfloat16),
            pltpu.VMEM(block, jnp.bfloat16),
            pltpu.VMEM((CHUNKS, 4, 4, 8, DIM), jnp.float32),
            pltpu.VMEM((4, CHUNKS, 2, 2, 2, TOK, DIM), jnp.bfloat16),
            dma((CHUNKS, 4)),
            dma((3, CHUNKS, 4)),
            dma((3, CHUNKS, 4)),
            dma((2, CHUNKS, 2, 2)),
            dma((2, CHUNKS, 2, 2)),
            dma((2, CHUNKS, 2, 2)),
            dma((2, CHUNKS, 2, 2)),
            dma((CHUNKS, 2)),
            dma((CHUNKS, 2)),
            dma((CHUNKS, 2)),
            dma((CHUNKS, 2)),
            dma((4, CHUNKS)),
            dma((3, 4, CHUNKS)),
            dma((3, 4, CHUNKS)),
        ],
        compiler_params=pltpu.CompilerParams(
            collective_id=0, has_side_effects=True, vmem_limit_bytes=48 * 1024 * 1024
        ),
    )(queries, keys, values, grad_out)


def solution(mesh):
    spec = P("ta", "gy", "gx", None, None)
    return jax.shard_map(
        body, mesh=mesh, in_specs=(spec,) * 4, out_specs=(spec,) * 4, check_vma=False
    )
```

profile of v0, /device:TPU:1, one launch (start us, length us, event | category | flops | bytes accessed | tf_op | source)
XLA Modules:
  0.0 79.0 jit_solution(832560169253933753)
XLA Ops:
  0.6 0.0 copy-start
  0.6 1.0 %copy-done = bf16[1,1,2,64,1536]{4,3,2,1,0:T(8,128)(2,1)S(1)} copy-done((bf16[1,1,2,64,1536]{4,3,2,1,0:T(8,128)(2,1)S(1)}, bf16[1,1,2,64,1536]{4,3,2,1,0:T(8,128)(2,1)}, u32[]{:S(2)}) %copy-start) | copy-done | bytes 393240
  1.6 0.0 copy-start.1
  1.6 1.0 %copy-done.1 = bf16[1,1,2,64,1536]{4,3,2,1,0:T(8,128)(2,1)S(1)} copy-done((bf16[1,1,2,64,1536]{4,3,2,1,0:T(8,128)(2,1)S(1)}, bf16[1,1,2,64,1536]{4,3,2,1,0:T(8,128)(2,1)}, u32[]{:S(2)}) %copy-start.1) | copy-done | bytes 393240
  2.6 0.0 copy-start.2
  2.6 1.0 %copy-done.2 = bf16[1,1,2,64,1536]{4,3,2,1,0:T(8,128)(2,1)S(1)} copy-done((bf16[1,1,2,64,1536]{4,3,2,1,0:T(8,128)(2,1)S(1)}, bf16[1,1,2,64,1536]{4,3,2,1,0:T(8,128)(2,1)}, u32[]{:S(2)}) %copy-start.2) | copy-done | bytes 393240
  3.6 0.0 copy-start.3
  3.6 1.0 %copy-done.3 = bf16[1,1,2,64,1536]{4,3,2,1,0:T(8,128)(2,1)S(1)} copy-done((bf16[1,1,2,64,1536]{4,3,2,1,0:T(8,128)(2,1)S(1)}, bf16[1,1,2,64,1536]{4,3,2,1,0:T(8,128)(2,1)}, u32[]{:S(2)}) %copy-start.3) | copy-done | bytes 393240
  4.6 71.4 %shard_map.75 = (bf16[1,1,2,64,1536]{4,3,2,1,0:T(8,128)(2,1)S(1)}, bf16[1,1,2,64,1536]{4,3,2,1,0:T(8,128)(2,1)S(1)}, bf16[1,1,2,64,1536]{4,3,2,1,0:T(8,128)(2,1)S(1)}, bf16[1,1,2,64,1536]{4,3,2,1,0:T(8,128)(2,1)S(1)}) custom-call(bf16[1,1,2,64,1536]{4,3,2,1,0:T(8,128)(2,1)S(1)} %copy-done, bf16[1,1,2,64,1536]{4,3,2,1,0:T(8,128)(2,1)S(1)} %copy-done.1, ...), custom_call_target="tpu_custom_call" | custom-call | tf_op jit(solution)/shard_map/pallas_call | solution.py:329
  76.0 0.7 copy.12
  76.7 0.7 copy.13
  77.5 0.7 copy.14
  78.2 0.7 copy.15
Async XLA Ops:
  0.6 1.0 %copy-start = (bf16[1,1,2,64,1536]{4,3,2,1,0:T(8,128)(2,1)S(1)}, bf16[1,1,2,64,1536]{4,3,2,1,0:T(8,128)(2,1)}, u32[]{:S(2)}) copy-start(bf16[1,1,2,64,1536]{4,3,2,1,0:T(8,128)(2,1)} %q_in.1) | copy-start | bytes 1179652
  1.6 1.0 %copy-start.1 = (bf16[1,1,2,64,1536]{4,3,2,1,0:T(8,128)(2,1)S(1)}, bf16[1,1,2,64,1536]{4,3,2,1,0:T(8,128)(2,1)}, u32[]{:S(2)}) copy-start(bf16[1,1,2,64,1536]{4,3,2,1,0:T(8,128)(2,1)} %k_in.1) | copy-start | bytes 1179652
  2.6 1.0 %copy-start.2 = (bf16[1,1,2,64,1536]{4,3,2,1,0:T(8,128)(2,1)S(1)}, bf16[1,1,2,64,1536]{4,3,2,1,0:T(8,128)(2,1)}, u32[]{:S(2)}) copy-start(bf16[1,1,2,64,1536]{4,3,2,1,0:T(8,128)(2,1)} %v_in.1) | copy-start | bytes 1179652
  3.6 1.0 %copy-start.3 = (bf16[1,1,2,64,1536]{4,3,2,1,0:T(8,128)(2,1)S(1)}, bf16[1,1,2,64,1536]{4,3,2,1,0:T(8,128)(2,1)}, u32[]{:S(2)}) copy-start(bf16[1,1,2,64,1536]{4,3,2,1,0:T(8,128)(2,1)} %g_in.1) | copy-start | bytes 1179652
where the time goes:
time: 79.4 us; the launch traced here: 79 us
  Pallas kernels  71.4 us (90%)
  local copies, waits for them, and re-layouts  6.96 us (9%)
    pallas_call x1, Pallas kernels, body(): pl.pallas_call(kernel, out_shape=[jax.ShapeDtypeStruct(queries.shape, jnp...  71.4 us
    unnamed x12, local copies, waits for them, and re-layouts  6.96 us

commit v1 on v0

v1 whole, which is shorter than its diff:
```python
import jax
import jax.numpy as jnp
from jax import lax
from jax.experimental import pallas as pl
from jax.experimental.pallas import tpu as pltpu
from jax.sharding import PartitionSpec as P

MESH = pl.DeviceIdType.MESH
DIM = 128
TOK = 64
CHUNKS = 3
FACTOR = DIM ** -0.5
SCALE = FACTOR * 1.4426950408889634
FAR = 1e30
FRAMES = 16
TCOLS = 16
NT = (((1,), (1,)), ((), ()))
NN = (((1,), (0,)), ((), ()))


def dot_nt(a, b):
    return lax.dot_general(a, b, NT, preferred_element_type=jnp.float32)


def dot_nn(a, b):
    return lax.dot_general(a, b, NN, preferred_element_type=jnp.float32)


def kernel(
    q_in, k_in, v_in, g_in, out_o, out_dq, out_dk, out_dv,
    kv, qg, st, stage,
    local_sem, in_send, in_recv, y_send, y_recv, z_send, z_recv,
    cy_send, cy_recv, cz_send, cz_recv, st_send, st_recv, keep_sem, back_send, back_recv,
):
    ta = lax.axis_index("ta")
    xl = lax.axis_index("gy")
    gx = lax.axis_index("gx")
    z, core = ta // 2, ta % 2
    xh = gx // 4
    side = (xl + xh) % 2

    def along_y(step):
        other = (gx + step + 8) % 8
        return (ta, (side + other // 4) % 2, other)

    def along_z(step):
        return (((z + step + 8) % 8) * 2 + core, xl, gx)

    peers = ((0, 1), (1, 0), (1, 1))

    def peer_id(p):
        dx, dc = peers[p]
        return (z * 2 + (core + dc) % 2, (xl + dx) % 2, gx)

    def peer_group(p):
        dx, dc = peers[p]
        return 2 * ((side + dx) % 2) + (core + dc) % 2

    my_group = 2 * side + core
    around = ((1, 0), (-1, 0), (0, 1), (0, -1), (1, 1), (1, -1), (-1, 1), (-1, -1))
    around_ids = tuple((along_z(dz)[0], *along_y(dy)[1:]) for dy, dz in around)
    y_ids, z_ids = around_ids[:2], around_ids[2:4]

    barrier = pltpu.get_barrier_semaphore()
    for target in (peer_id(0), peer_id(1), peer_id(2), *around_ids):
        pl.semaphore_signal(barrier, inc=1, device_id=target, device_id_type=MESH)
    pl.semaphore_wait(barrier, 11)

    def lanes(group, j):
        return pl.ds(pl.multiple_of((group * CHUNKS + j) * DIM, DIM), DIM)

    sources = (k_in, v_in, q_in, g_in)
    results = (out_o, out_dq, out_dk, out_dv)

    def slot(t, j):
        held = kv if t < 2 else qg
        return held.at[j, t % 2, pl.ds(1, 2), 1 + core, xl]

    def local_copy(j, t):
        return pltpu.make_async_copy(
            sources[t].at[0, 0, :, :, lanes(my_group, j)], slot(t, j), local_sem.at[j, t]
        )

    def in_copy(p, j, t):
        return pltpu.make_async_remote_copy(
            src_ref=sources[t].at[0, 0, :, :, lanes(peer_group(p), j)],
            dst_ref=slot(t, j),
            send_sem=in_send.at[p, j, t],
            recv_sem=in_recv.at[p, j, t],
            device_id=peer_id(p),
            device_id_type=MESH,
        )

    def remote(src, dst, send, recv, target):
        return pltpu.make_async_remote_copy(
            src_ref=src, dst_ref=dst, send_sem=send, recv_sem=recv,
            device_id=target, device_id_type=MESH,
        )

    def edge_y(h, j, w, d):
        row = (xl + w) % 2
        held = (kv, qg)[h]
        return remote(
            held.at[j, :, 2 - d, pl.ds(1, 2), row], held.at[j, :, 3 * d, pl.ds(1, 2), row],
            y_send.at[h, j, w, d], y_recv.at[h, j, row, d], y_ids[d],
        )

    def edge_z(h, j, w, d):
        row = (xl + w) % 2
        held = (kv, qg)[h]
        return remote(
            held.at[j, :, pl.ds(1, 2), 2 - d, row], held.at[j, :, pl.ds(1, 2), 3 * d, row],
            z_send.at[h, j, w, d], z_recv.at[h, j, row, d], z_ids[d],
        )

    def corner_z(j, e, d):
        return remote(
            kv.at[j, :, 3 * e, 2 - d], kv.at[j, :, 3 * e, 3 * d],
            cz_send.at[j, e, d], cz_recv.at[j, e, d], z_ids[d],
        )

    def corner_y(j, e, d):
        return remote(
            qg.at[j, :, 2 - d, 3 * e], qg.at[j, :, 3 * d, 3 * e],
            cy_send.at[j, e, d], cy_recv.at[j, e, d], y_ids[d],
        )

    def stat_copy(j, n):
        dy, dz = around[n]
        cols = {0: (pl.ds(1, 2), pl.ds(1, 2)), 1: (2, 0), -1: (1, 3)}[dy]
        frames = {0: (pl.ds(1, 2), pl.ds(1, 2)), 1: (2, 0), -1: (1, 3)}[dz]
        return remote(
            st.at[j, cols[0], frames[0]], st.at[j, cols[1], frames[1]],
            st_send.at[j, n], st_recv.at[j, n], around_ids[n],
        )

    def keep_copy(t, j):
        return pltpu.make_async_copy(
            stage.at[t, j, :, core, xl], results[t].at[0, 0, :, :, lanes(my_group, j)],
            keep_sem.at[t, j],
        )

    def back_copy(p, t, j):
        dx, dc = peers[p]
        return remote(
            stage.at[t, j, :, (core + dc) % 2, (xl + dx) % 2],
            results[t].at[0, 0, :, :, lanes(my_group, j)],
            back_send.at[p, t, j], back_recv.at[p, t, j], peer_id(p),
        )

    for j in range(CHUNKS):
        for t in range(4):
            local_copy(j, t).start()
            in_copy(0, j, t).start()
    for j in range(CHUNKS):
        for t in range(4):
            for p in (1, 2):
                in_copy(p, j, t).start()

    def first_hops(j, w):
        for h in range(2):
            for t in (2 * h, 2 * h + 1):
                if w == 0:
                    local_copy(j, t).wait()
                    in_copy(0, j, t).wait_recv()
                else:
                    in_copy(1, j, t).wait_recv()
                    in_copy(2, j, t).wait_recv()
            for d in range(2):
                edge_y(h, j, w, d).start()
                edge_z(h, j, w, d).start()

    def second_hops(j):
        for d in range(2):
            for w in range(2):
                edge_y(0, j, w, d).wait_recv()
        for e in range(2):
            for d in range(2):
                corner_z(j, e, d).start()
        for d in range(2):
            for w in range(2):
                edge_z(1, j, w, d).wait_recv()
        for e in range(2):
            for d in range(2):
                corner_y(j, e, d).start()

    def in_grid(c, f, dc, df):
        col = 2 * gx + c + dc - 1
        frame = 2 * z + f + df - 1
        return (col >= 0) & (col < TCOLS) & (frame >= 0) & (frame < FRAMES)

    lane = lax.broadcasted_iota(jnp.int32, (DIM, DIM), 1)

    def pair(half0, half1):
        blank = jnp.zeros((2 * TOK, DIM), half0.dtype)
        return jnp.concatenate(
            [jnp.concatenate([half0, blank], axis=1), jnp.concatenate([blank, half1], axis=1)],
            axis=0,
        )

    def halves(x):
        return x[:2 * TOK, :3 * DIM], x[2 * TOK:, DIM:]

    def query_block(j, c):
        q = qg[j, 0, 1 + c, 1:3].reshape(4 * TOK, DIM)
        g = qg[j, 1, 1 + c, 1:3].reshape(4 * TOK, DIM)
        scores = [[], []]
        for dc in range(3):
            s = dot_nt(q, kv[j, 0, c + dc].reshape(8 * TOK, DIM))
            for f, part in enumerate(halves(s)):
                scores[f].append(jnp.concatenate([
                    part[:, df * DIM:(df + 1) * DIM] * SCALE
                    + jnp.where(in_grid(c, f, dc, df), 0.0, -FAR)
                    for df in range(3)
                ], axis=1))
        tops, powers, totals = [], [], []
        for f in range(2):
            top = jnp.maximum(jnp.maximum(scores[f][0], scores[f][1]), scores[f][2])
            top = jnp.max(top, axis=1, keepdims=True)
            p = [jnp.exp2(s - top) for s in scores[f]]
            tops.append(top)
            powers.append(p)
            totals.append(jnp.sum(p[0] + p[1] + p[2], axis=1, keepdims=True))
        top = jnp.concatenate(tops, axis=0)
        total = jnp.concatenate(totals, axis=0)
        scale = 1.0 / total
        att = jnp.zeros((4 * TOK, DIM), jnp.float32)
        for dc in range(3):
            v = kv[j, 1, c + dc].reshape(8 * TOK, DIM)
            att += dot_nn(pair(*(powers[f][dc].astype(jnp.bfloat16) for f in range(2))), v)
        att = (att * scale).astype(jnp.bfloat16)
        dots = jnp.sum(g.astype(jnp.float32) * att.astype(jnp.float32), axis=1, keepdims=True)
        grad = jnp.zeros((4 * TOK, DIM), jnp.float32)
        for dc in range(3):
            k = kv[j, 0, c + dc].reshape(8 * TOK, DIM)
            v = kv[j, 1, c + dc].reshape(8 * TOK, DIM)
            pulls = halves(dot_nt(g, v))
            slopes = (
                (powers[f][dc] * (pulls[f] - dots[f * 2 * TOK:(f + 1) * 2 * TOK])).astype(jnp.bfloat16)
                for f in range(2)
            )
            grad += dot_nn(pair(*slopes), k)
        grad = (grad * (scale * FACTOR)).astype(jnp.bfloat16)
        stage[0, j, c] = att.reshape(2, 2, TOK, DIM)
        stage[1, j, c] = grad.reshape(2, 2, TOK, DIM)
        level = top + jnp.log2(total)
        for f in range(2):
            cut = slice(f * 2 * TOK, (f + 1) * 2 * TOK)
            st[j, 1 + c, 1 + f] = jnp.transpose(jnp.where(lane == 0, level[cut], dots[cut]))[:8]

    def key_block(j, c):
        k = kv[j, 0, 1 + c, 1:3].reshape(4 * TOK, DIM)
        v = kv[j, 1, 1 + c, 1:3].reshape(4 * TOK, DIM)
        grad_k = jnp.zeros((4 * TOK, DIM), jnp.float32)
        grad_v = jnp.zeros((4 * TOK, DIM), jnp.float32)
        for dc in range(3):
            q = qg[j, 0, c + dc].reshape(8 * TOK, DIM)
            g = qg[j, 1, c + dc].reshape(8 * TOK, DIM)
            s = halves(dot_nt(k, q))
            pulls = halves(dot_nt(v, g))
            weights, slopes = [], []
            for f in range(2):
                ws, ss = [], []
                for df in range(3):
                    tile = st[j, c + dc, f + df]
                    level = jnp.where(in_grid(c, f, dc, df), tile[0:1], FAR)
                    cut = slice(df * DIM, (df + 1) * DIM)
                    w = jnp.exp2(s[f][:, cut] * SCALE - level)
                    ws.append(w.astype(jnp.bfloat16))
                    ss.append((w * (pulls[f][:, cut] - tile[1:2])).astype(jnp.bfloat16))
                weights.append(jnp.concatenate(ws, axis=1))
                slopes.append(jnp.concatenate(ss, axis=1))
            grad_v += dot_nn(pair(*weights), g)
            grad_k += dot_nn(pair(*slopes), q)
        stage[2, j, c] = (grad_k * FACTOR).astype(jnp.bfloat16).reshape(2, 2, TOK, DIM)
        stage[3, j, c] = grad_v.astype(jnp.bfloat16).reshape(2, 2, TOK, DIM)

    def blocks(run, j):
        def one(c, carry):
            run(j, c)
            return carry

        lax.fori_loop(0, 2, one, 0)

    def send_back(j, ts):
        for t in ts:
            for p in (1, 2, 0):
                back_copy(p, t, j).start()
            keep_copy(t, j).start()

    def query_side(j):
        for d in range(2):
            for w in range(2):
                edge_z(0, j, w, d).wait_recv()
        for e in range(2):
            for d in range(2):
                corner_z(j, e, d).wait_recv()
        blocks(query_block, j)
        for n in range(8):
            stat_copy(j, n).start()
        send_back(j, (0, 1))

    def key_side(j):
        for d in range(2):
            for w in range(2):
                edge_y(1, j, w, d).wait_recv()
        for e in range(2):
            for d in range(2):
                corner_y(j, e, d).wait_recv()
        for n in range(8):
            stat_copy(j, n).wait_recv()
        blocks(key_block, j)
        send_back(j, (2, 3))

    first_hops(0, 0)
    first_hops(1, 0)
    first_hops(0, 1)
    first_hops(2, 0)
    second_hops(0)
    first_hops(1, 1)
    first_hops(2, 1)
    second_hops(1)
    query_side(0)
    second_hops(2)
    query_side(1)
    key_side(0)
    query_side(2)
    key_side(1)
    key_side(2)
    for j in range(CHUNKS):
        for t in range(4):
            for p in range(3):
                in_copy(p, j, t).wait_send()
        for d in range(2):
            for w in range(2):
                for h in range(2):
                    edge_y(h, j, w, d).wait_send()
                    edge_z(h, j, w, d).wait_send()
            for e in range(2):
                corner_z(j, e, d).wait_send()
                corner_y(j, e, d).wait_send()
        for n in range(8):
            stat_copy(j, n).wait_send()
        for t in range(4):
            keep_copy(t, j).wait()
            for p in range(3):
                back_copy(p, t, j).wait_send()
                back_copy(p, t, j).wait_recv()


def drain(*refs):
    held, out, sem = refs[:4], refs[4:8], refs[8]
    copies = [pltpu.make_async_copy(held[t], out[t], sem.at[t]) for t in range(4)]
    for copy in copies:
        copy.start()
    for copy in copies:
        copy.wait()


def body(queries, keys, values, grad_out):
    dma = pltpu.SemaphoreType.DMA
    block = (CHUNKS, 2, 4, 4, 2, TOK, DIM)
    held = pl.pallas_call(
        kernel,
        out_shape=[jax.ShapeDtypeStruct(queries.shape, jnp.bfloat16)] * 4,
        in_specs=[pl.BlockSpec(memory_space=pl.ANY)] * 4,
        out_specs=[pl.BlockSpec(memory_space=pl.ANY)] * 4,
        scratch_shapes=[
            pltpu.VMEM(block, jnp.bfloat16),
            pltpu.VMEM(block, jnp.bfloat16),
            pltpu.VMEM((CHUNKS, 4, 4, 8, DIM), jnp.float32),
            pltpu.VMEM((4, CHUNKS, 2, 2, 2, TOK, DIM), jnp.bfloat16),
            dma((CHUNKS, 4)),
            dma((3, CHUNKS, 4)),
            dma((3, CHUNKS, 4)),
            dma((2, CHUNKS, 2, 2)),
            dma((2, CHUNKS, 2, 2)),
            dma((2, CHUNKS, 2, 2)),
            dma((2, CHUNKS, 2, 2)),
            dma((CHUNKS, 2, 2)),
            dma((CHUNKS, 2, 2)),
            dma((CHUNKS, 2, 2)),
            dma((CHUNKS, 2, 2)),
            dma((CHUNKS, 8)),
            dma((CHUNKS, 8)),
            dma((4, CHUNKS)),
            dma((3, 4, CHUNKS)),
            dma((3, 4, CHUNKS)),
        ],
        compiler_params=pltpu.CompilerParams(
            collective_id=0, has_side_effects=True, vmem_limit_bytes=40*1024*1024
        ),
    )(*(pltpu.with_memory_space_constraint(a, pltpu.HBM) for a in (queries, keys, values, grad_out)))
    return pl.pallas_call(
        drain,
        out_shape=[jax.ShapeDtypeStruct(queries.shape, jnp.bfloat16)] * 4,
        in_specs=[pl.BlockSpec(memory_space=pl.ANY)] * 4,
        out_specs=[pl.BlockSpec(memory_space=pl.ANY)] * 4,
        scratch_shapes=[dma((4,))],
        compiler_params=pltpu.CompilerParams(vmem_limit_bytes=1024 * 1024),
    )(*held)


def solution(mesh):
    spec = P("ta", "gy", "gx", None, None)
    return jax.shard_map(
        body, mesh=mesh, in_specs=(spec,) * 4, out_specs=(spec,) * 4, check_vma=False
    )
```

time: 79.4 us -> 61.4 us (0.77)
  Pallas kernels: 71.4 us -> 60.6 us
  local copies, waits for them, and re-layouts: 6.96 us -> 0 us
    pallas_call x1, Pallas kernels: 71.4 us -> 59.4 us  [body(): pl.pallas_call(kernel, out_shape=[jax.ShapeDtypeStruct(queries.shape, jnp...]
    unnamed x12 -> x0, local copies, waits for them, and re-layouts: 6.96 us -> none
    pallas_call x0 -> x1, Pallas kernels: none -> 1.17 us  [body(): pl.pallas_call(drain, out_shape=[jax.ShapeDtypeStruct(queries.shape, jnp....]
where the time goes in v1:
time: 61.4 us; the launch traced here: 61.2 us
  Pallas kernels  60.6 us (99%)
  between operations  0.64 us (1%)
    pallas_call x1, Pallas kernels, body(): pl.pallas_call(kernel, out_shape=[jax.ShapeDtypeStruct(queries.shape, jnp...  59.4 us

profile of v1, /device:TPU:1, one launch (start us, length us, event | category | flops | bytes accessed | tf_op | source)
XLA Modules:
  0.0 61.2 jit_solution(18207039555174112620)
XLA Ops:
  0.6 59.4 %shard_map.75 = (bf16[1,1,2,64,1536]{4,3,2,1,0:T(8,128)(2,1)S(1)}, bf16[1,1,2,64,1536]{4,3,2,1,0:T(8,128)(2,1)S(1)}, bf16[1,1,2,64,1536]{4,3,2,1,0:T(8,128)(2,1)S(1)}, bf16[1,1,2,64,1536]{4,3,2,1,0:T(8,128)(2,1)S(1)}) custom-call(bf16[1,1,2,64,1536]{4,3,2,1,0:T(8,128)(2,1)} %q_in.1, bf16[1,1,2,64,1536]{4,3,2,1,0:T(8,128)(2,1)} %k_in.1, ...), custom_call_target="tpu_custom_call" | custom-call | tf_op jit(solution)/shard_map/pallas_call | solution.py:363
  60.1 1.2 %shard_map.76 = (bf16[1,1,2,64,1536]{4,3,2,1,0:T(8,128)(2,1)}, bf16[1,1,2,64,1536]{4,3,2,1,0:T(8,128)(2,1)}, bf16[1,1,2,64,1536]{4,3,2,1,0:T(8,128)(2,1)}, bf16[1,1,2,64,1536]{4,3,2,1,0:T(8,128)(2,1)}) custom-call(bf16[1,1,2,64,1536]{4,3,2,1,0:T(8,128)(2,1)S(1)} %get-tuple-element.8.refs_0_, bf16[1,1,2,64,1536]{4,3,2,1,0:T(8,128)(2,1)S(1)} %get-tuple-element.9.refs_1_, ...), custom_call_target="tpu_custom_call" | custom-call | tf_op jit(solution)/shard_map/pallas_call | solution.py:394

commit v2 on v1

--- a/solution.py
+++ b/solution.py
@@ -29,8 +29,8 @@
 def kernel(
     q_in, k_in, v_in, g_in, out_o, out_dq, out_dk, out_dv,
     kv, qg, st, stage,
-    local_sem, in_send, in_recv, y_send, y_recv, z_send, z_recv,
-    cy_send, cy_recv, cz_send, cz_recv, st_send, st_recv, keep_sem, back_send, back_recv,
+    in_send, in_recv, edge_send, y_recv, z_recv, corner_send, cy_recv, cz_recv,
+    st_send, st_recv, back_send, back_recv,
 ):
     ta = lax.axis_index("ta")
     xl = lax.axis_index("gy")
@@ -78,15 +78,15 @@
 
     def local_copy(j, t):
         return pltpu.make_async_copy(
-            sources[t].at[0, 0, :, :, lanes(my_group, j)], slot(t, j), local_sem.at[j, t]
+            sources[t].at[0, 0, :, :, lanes(my_group, j)], slot(t, j), in_recv.at[j, 0, t // 2]
         )
 
     def in_copy(p, j, t):
         return pltpu.make_async_remote_copy(
             src_ref=sources[t].at[0, 0, :, :, lanes(peer_group(p), j)],
             dst_ref=slot(t, j),
-            send_sem=in_send.at[p, j, t],
-            recv_sem=in_recv.at[p, j, t],
+            send_sem=in_send,
+            recv_sem=in_recv.at[j, min(p, 1), t // 2],
             device_id=peer_id(p),
             device_id_type=MESH,
         )
@@ -102,7 +102,7 @@
         held = (kv, qg)[h]
         return remote(
             held.at[j, :, 2 - d, pl.ds(1, 2), row], held.at[j, :, 3 * d, pl.ds(1, 2), row],
-            y_send.at[h, j, w, d], y_recv.at[h, j, row, d], y_ids[d],
+            edge_send, y_recv.at[h, j], y_ids[d],
         )
 
     def edge_z(h, j, w, d):
@@ -110,19 +110,19 @@
         held = (kv, qg)[h]
         return remote(
             held.at[j, :, pl.ds(1, 2), 2 - d, row], held.at[j, :, pl.ds(1, 2), 3 * d, row],
-            z_send.at[h, j, w, d], z_recv.at[h, j, row, d], z_ids[d],
+            edge_send, z_recv.at[h, j], z_ids[d],
         )
 
     def corner_z(j, e, d):
         return remote(
             kv.at[j, :, 3 * e, 2 - d], kv.at[j, :, 3 * e, 3 * d],
-            cz_send.at[j, e, d], cz_recv.at[j, e, d], z_ids[d],
+            corner_send, cz_recv.at[j], z_ids[d],
         )
 
     def corner_y(j, e, d):
         return remote(
             qg.at[j, :, 2 - d, 3 * e], qg.at[j, :, 3 * d, 3 * e],
-            cy_send.at[j, e, d], cy_recv.at[j, e, d], y_ids[d],
+            corner_send, cy_recv.at[j], y_ids[d],
         )
 
     def stat_copy(j, n):
@@ -131,13 +131,13 @@
         frames = {0: (pl.ds(1, 2), pl.ds(1, 2)), 1: (2, 0), -1: (1, 3)}[dz]
         return remote(
             st.at[j, cols[0], frames[0]], st.at[j, cols[1], frames[1]],
-            st_send.at[j, n], st_recv.at[j, n], around_ids[n],
+            st_send, st_recv.at[j], around_ids[n],
         )
 
     def keep_copy(t, j):
         return pltpu.make_async_copy(
             stage.at[t, j, :, core, xl], results[t].at[0, 0, :, :, lanes(my_group, j)],
-            keep_sem.at[t, j],
+            back_recv,
         )
 
     def back_copy(p, t, j):
@@ -145,7 +145,7 @@
         return remote(
             stage.at[t, j, :, (core + dc) % 2, (xl + dx) % 2],
             results[t].at[0, 0, :, :, lanes(my_group, j)],
-            back_send.at[p, t, j], back_recv.at[p, t, j], peer_id(p),
+            back_send, back_recv, peer_id(p),
         )
 
     for j in range(CHUNKS):
@@ -157,29 +157,23 @@
             for p in (1, 2):
                 in_copy(p, j, t).start()
 
+    def settle(sem, like):
+        pltpu.make_async_copy(like, like, sem).wait()
+
     def first_hops(j, w):
+        row = (xl + w) % 2
         for h in range(2):
-            for t in (2 * h, 2 * h + 1):
-                if w == 0:
-                    local_copy(j, t).wait()
-                    in_copy(0, j, t).wait_recv()
-                else:
-                    in_copy(1, j, t).wait_recv()
-                    in_copy(2, j, t).wait_recv()
+            settle(in_recv.at[j, w, h], (kv, qg)[h].at[j, :, pl.ds(1, 2), pl.ds(1, 2), row])
             for d in range(2):
                 edge_y(h, j, w, d).start()
                 edge_z(h, j, w, d).start()
 
     def second_hops(j):
-        for d in range(2):
-            for w in range(2):
-                edge_y(0, j, w, d).wait_recv()
+        settle(y_recv.at[0, j], kv.at[j, :, pl.ds(0, 2), pl.ds(1, 2)])
         for e in range(2):
             for d in range(2):
                 corner_z(j, e, d).start()
-        for d in range(2):
-            for w in range(2):
-                edge_z(1, j, w, d).wait_recv()
+        settle(z_recv.at[1, j], qg.at[j, :, pl.ds(1, 2), pl.ds(0, 2)])
         for e in range(2):
             for d in range(2):
                 corner_y(j, e, d).start()
@@ -289,26 +283,17 @@
             keep_copy(t, j).start()
 
     def query_side(j):
-        for d in range(2):
-            for w in range(2):
-                edge_z(0, j, w, d).wait_recv()
-        for e in range(2):
-            for d in range(2):
-                corner_z(j, e, d).wait_recv()
+        settle(z_recv.at[0, j], kv.at[j, :, pl.ds(1, 2), pl.ds(0, 2)])
+        settle(cz_recv.at[j], kv.at[j, :, pl.ds(0, 2), pl.ds(0, 2)])
         blocks(query_block, j)
         for n in range(8):
             stat_copy(j, n).start()
         send_back(j, (0, 1))
 
     def key_side(j):
-        for d in range(2):
-            for w in range(2):
-                edge_y(1, j, w, d).wait_recv()
-        for e in range(2):
-            for d in range(2):
-                corner_y(j, e, d).wait_recv()
-        for n in range(8):
-            stat_copy(j, n).wait_recv()
+        settle(y_recv.at[1, j], qg.at[j, :, pl.ds(0, 2), pl.ds(1, 2)])
+        settle(cy_recv.at[j], qg.at[j, :, pl.ds(0, 2), pl.ds(0, 2)])
+        settle(st_recv.at[j], st.at[j, pl.ds(0, 3)])
         blocks(key_block, j)
         send_back(j, (2, 3))
 
@@ -327,25 +312,12 @@
     query_side(2)
     key_side(1)
     key_side(2)
-    for j in range(CHUNKS):
-        for t in range(4):
-            for p in range(3):
-                in_copy(p, j, t).wait_send()
-        for d in range(2):
-            for w in range(2):
-                for h in range(2):
-                    edge_y(h, j, w, d).wait_send()
-                    edge_z(h, j, w, d).wait_send()
-            for e in range(2):
-                corner_z(j, e, d).wait_send()
-                corner_y(j, e, d).wait_send()
-        for n in range(8):
-            stat_copy(j, n).wait_send()
-        for t in range(4):
-            keep_copy(t, j).wait()
-            for p in range(3):
-                back_copy(p, t, j).wait_send()
-                back_copy(p, t, j).wait_recv()
+    settle(in_send, kv.at[:, :, pl.ds(0, 3), :, 0])
+    settle(edge_send, kv)
+    settle(corner_send, kv.at[:, :, pl.ds(0, 2)])
+    settle(st_send, st.at[:, pl.ds(0, 3)])
+    settle(back_send, kv.at[:, :, pl.ds(0, 3), :, 0])
+    settle(back_recv, kv.at[:, :, pl.ds(0, 2)])
 
 
 def drain(*refs):
@@ -370,22 +342,18 @@
             pltpu.VMEM(block, jnp.bfloat16),
             pltpu.VMEM((CHUNKS, 4, 4, 8, DIM), jnp.float32),
             pltpu.VMEM((4, CHUNKS, 2, 2, 2, TOK, DIM), jnp.bfloat16),
-            dma((CHUNKS, 4)),
-            dma((3, CHUNKS, 4)),
-            dma((3, CHUNKS, 4)),
-            dma((2, CHUNKS, 2, 2)),
-            dma((2, CHUNKS, 2, 2)),
-            dma((2, CHUNKS, 2, 2)),
-            dma((2, CHUNKS, 2, 2)),
+            dma(()),
             dma((CHUNKS, 2, 2)),
-            dma((CHUNKS, 2, 2)),
-            dma((CHUNKS, 2, 2)),
-            dma((CHUNKS, 2, 2)),
-            dma((CHUNKS, 8)),
-            dma((CHUNKS, 8)),
-            dma((4, CHUNKS)),
-            dma((3, 4, CHUNKS)),
-            dma((3, 4, CHUNKS)),
+            dma(()),
+            dma((2, CHUNKS)),
+            dma((2, CHUNKS)),
+            dma(()),
+            dma((CHUNKS,)),
+            dma((CHUNKS,)),
+            dma(()),
+            dma((CHUNKS,)),
+            dma(()),
+            dma(()),
         ],
         compiler_params=pltpu.CompilerParams(
             collective_id=0, has_side_effects=True, vmem_limit_bytes=40*1024*1024

time: 61.4 us -> 58.5 us (0.953)
  Pallas kernels: 60.6 us -> 57.7 us
    pallas_call x1, Pallas kernels: 59.4 us -> 56.6 us  [body(): pl.pallas_call(kernel, out_shape=[jax.ShapeDtypeStruct(queries.shape, jnp...]
where the time goes in v2:
time: 58.5 us; the launch traced here: 58.4 us
  Pallas kernels  57.7 us (99%)
  between operations  0.64 us (1%)
    pallas_call x1, Pallas kernels, body(): pl.pallas_call(kernel, out_shape=[jax.ShapeDtypeStruct(queries.shape, jnp...  56.6 us
    pallas_call x1, Pallas kernels, body(): pl.pallas_call(drain, out_shape=[jax.ShapeDtypeStruct(queries.shape, jnp....  1.17 us

profile of v2, /device:TPU:1, one launch (start us, length us, event | category | flops | bytes accessed | tf_op | source)
XLA Modules:
  0.0 58.4 jit_solution(11203479230432045544)
XLA Ops:
  0.6 56.6 %shard_map.75 = (bf16[1,1,2,64,1536]{4,3,2,1,0:T(8,128)(2,1)S(1)}, bf16[1,1,2,64,1536]{4,3,2,1,0:T(8,128)(2,1)S(1)}, bf16[1,1,2,64,1536]{4,3,2,1,0:T(8,128)(2,1)S(1)}, bf16[1,1,2,64,1536]{4,3,2,1,0:T(8,128)(2,1)S(1)}) custom-call(bf16[1,1,2,64,1536]{4,3,2,1,0:T(8,128)(2,1)} %q_in.1, bf16[1,1,2,64,1536]{4,3,2,1,0:T(8,128)(2,1)} %k_in.1, ...), custom_call_target="tpu_custom_call" | custom-call | tf_op jit(solution)/shard_map/pallas_call | solution.py:335
  57.2 1.2 %shard_map.76 = (bf16[1,1,2,64,1536]{4,3,2,1,0:T(8,128)(2,1)}, bf16[1,1,2,64,1536]{4,3,2,1,0:T(8,128)(2,1)}, bf16[1,1,2,64,1536]{4,3,2,1,0:T(8,128)(2,1)}, bf16[1,1,2,64,1536]{4,3,2,1,0:T(8,128)(2,1)}) custom-call(bf16[1,1,2,64,1536]{4,3,2,1,0:T(8,128)(2,1)S(1)} %get-tuple-element.8.refs_0_, bf16[1,1,2,64,1536]{4,3,2,1,0:T(8,128)(2,1)S(1)} %get-tuple-element.9.refs_1_, ...), custom_call_target="tpu_custom_call" | custom-call | tf_op jit(solution)/shard_map/pallas_call | solution.py:362

commit v3 on v2

--- a/solution.py
+++ b/solution.py
@@ -1,3 +1,5 @@
+import functools
+
 import jax
 import jax.numpy as jnp
 from jax import lax
@@ -134,17 +136,17 @@
             st_send, st_recv.at[j], around_ids[n],
         )
 
-    def keep_copy(t, j):
+    def keep_copy(t, j, c):
         return pltpu.make_async_copy(
-            stage.at[t, j, :, core, xl], results[t].at[0, 0, :, :, lanes(my_group, j)],
+            stage.at[t, j, c, core, xl], results[t].at[0, 0, c, :, lanes(my_group, j)],
             back_recv,
         )
 
-    def back_copy(p, t, j):
+    def back_copy(p, t, j, c):
         dx, dc = peers[p]
         return remote(
-            stage.at[t, j, :, (core + dc) % 2, (xl + dx) % 2],
-            results[t].at[0, 0, :, :, lanes(my_group, j)],
+            stage.at[t, j, c, (core + dc) % 2, (xl + dx) % 2],
+            results[t].at[0, 0, c, :, lanes(my_group, j)],
             back_send, back_recv, peer_id(p),
         )
 
@@ -178,124 +180,124 @@
             for d in range(2):
                 corner_y(j, e, d).start()
 
-    def in_grid(c, f, dc, df):
-        col = 2 * gx + c + dc - 1
-        frame = 2 * z + f + df - 1
+    def in_grid(ci, fi):
+        col = 2 * gx + ci - 1
+        frame = 2 * z + fi - 1
         return (col >= 0) & (col < TCOLS) & (frame >= 0) & (frame < FRAMES)
 
     lane = lax.broadcasted_iota(jnp.int32, (DIM, DIM), 1)
 
-    def pair(half0, half1):
-        blank = jnp.zeros((2 * TOK, DIM), half0.dtype)
-        return jnp.concatenate(
-            [jnp.concatenate([half0, blank], axis=1), jnp.concatenate([blank, half1], axis=1)],
-            axis=0,
-        )
-
-    def halves(x):
-        return x[:2 * TOK, :3 * DIM], x[2 * TOK:, DIM:]
+    own = (slice(0, 2 * TOK), slice(2 * TOK, 4 * TOK))
+
+    def inner(held, j, t, c):
+        return held[j, t, pl.ds(c, 3), 1:3].reshape(12 * TOK, DIM)
+
+    def outer(held, j, t, c, f):
+        return held[j, t, pl.ds(c, 3), 3 * f].reshape(6 * TOK, DIM)
+
+    def by_rows(make):
+        return jnp.concatenate([make(0), make(1)], axis=0)
+
+    def cuts(x):
+        return [x[:, n * DIM:(n + 1) * DIM] for n in range(x.shape[1] // DIM)]
+
+    def times(left, right, held, j, t, c):
+        return dot_nn(left, inner(held, j, t, c)) + by_rows(
+            lambda f: dot_nn(right[own[f]], outer(held, j, t, c, f))
+        )
+
+    def against(rows, held, j, t, c):
+        near = cuts(dot_nt(rows, inner(held, j, t, c)))
+        far = cuts(by_rows(lambda f: dot_nt(rows[own[f]], outer(held, j, t, c, f))))
+        return near + far
 
     def query_block(j, c):
         q = qg[j, 0, 1 + c, 1:3].reshape(4 * TOK, DIM)
         g = qg[j, 1, 1 + c, 1:3].reshape(4 * TOK, DIM)
-        scores = [[], []]
-        for dc in range(3):
-            s = dot_nt(q, kv[j, 0, c + dc].reshape(8 * TOK, DIM))
-            for f, part in enumerate(halves(s)):
-                scores[f].append(jnp.concatenate([
-                    part[:, df * DIM:(df + 1) * DIM] * SCALE
-                    + jnp.where(in_grid(c, f, dc, df), 0.0, -FAR)
-                    for df in range(3)
-                ], axis=1))
-        tops, powers, totals = [], [], []
-        for f in range(2):
-            top = jnp.maximum(jnp.maximum(scores[f][0], scores[f][1]), scores[f][2])
-            top = jnp.max(top, axis=1, keepdims=True)
-            p = [jnp.exp2(s - top) for s in scores[f]]
-            tops.append(top)
-            powers.append(p)
-            totals.append(jnp.sum(p[0] + p[1] + p[2], axis=1, keepdims=True))
-        top = jnp.concatenate(tops, axis=0)
-        total = jnp.concatenate(totals, axis=0)
+        bias = lambda ci, fi: jnp.where(in_grid(ci, fi), 0.0, -FAR)
+        scores = against(q, kv, j, 0, c)
+        for n in range(6):
+            scores[n] = scores[n] * SCALE + bias(c + n // 2, 1 + n % 2)
+        for n in range(3):
+            part = scores[6 + n] * SCALE
+            scores[6 + n] = by_rows(lambda f: part[own[f]] + bias(c + n, 3 * f))
+        top = functools.reduce(jnp.maximum, scores)
+        top = jnp.max(top, axis=1, keepdims=True)
+        powers = [jnp.exp2(s - top) for s in scores]
+        total = jnp.sum(functools.reduce(jnp.add, powers), axis=1, keepdims=True)
         scale = 1.0 / total
-        att = jnp.zeros((4 * TOK, DIM), jnp.float32)
-        for dc in range(3):
-            v = kv[j, 1, c + dc].reshape(8 * TOK, DIM)
-            att += dot_nn(pair(*(powers[f][dc].astype(jnp.bfloat16) for f in range(2))), v)
-        att = (att * scale).astype(jnp.bfloat16)
+
+        def rounded(parts):
+            parts = [p.astype(jnp.bfloat16) for p in parts]
+            return jnp.concatenate(parts[:6], axis=1), jnp.concatenate(parts[6:], axis=1)
+
+        att = (times(*rounded(powers), kv, j, 1, c) * scale).astype(jnp.bfloat16)
         dots = jnp.sum(g.astype(jnp.float32) * att.astype(jnp.float32), axis=1, keepdims=True)
-        grad = jnp.zeros((4 * TOK, DIM), jnp.float32)
-        for dc in range(3):
-            k = kv[j, 0, c + dc].reshape(8 * TOK, DIM)
-            v = kv[j, 1, c + dc].reshape(8 * TOK, DIM)
-            pulls = halves(dot_nt(g, v))
-            slopes = (
-                (powers[f][dc] * (pulls[f] - dots[f * 2 * TOK:(f + 1) * 2 * TOK])).astype(jnp.bfloat16)
-                for f in range(2)
-            )
-            grad += dot_nn(pair(*slopes), k)
+        pulls = against(g, kv, j, 1, c)
+        slopes = [p * (x - dots) for p, x in zip(powers, pulls)]
+        grad = times(*rounded(slopes), kv, j, 0, c)
         grad = (grad * (scale * FACTOR)).astype(jnp.bfloat16)
         stage[0, j, c] = att.reshape(2, 2, TOK, DIM)
         stage[1, j, c] = grad.reshape(2, 2, TOK, DIM)
         level = top + jnp.log2(total)
         for f in range(2):
-            cut = slice(f * 2 * TOK, (f + 1) * 2 * TOK)
-            st[j, 1 + c, 1 + f] = jnp.transpose(jnp.where(lane == 0, level[cut], dots[cut]))[:8]
+            both = jnp.where(lane == 0, level[own[f]], dots[own[f]])
+            st[j, 1 + c, 1 + f] = jnp.transpose(both)[:8]
 
     def key_block(j, c):
         k = kv[j, 0, 1 + c, 1:3].reshape(4 * TOK, DIM)
         v = kv[j, 1, 1 + c, 1:3].reshape(4 * TOK, DIM)
-        grad_k = jnp.zeros((4 * TOK, DIM), jnp.float32)
-        grad_v = jnp.zeros((4 * TOK, DIM), jnp.float32)
-        for dc in range(3):
-            q = qg[j, 0, c + dc].reshape(8 * TOK, DIM)
-            g = qg[j, 1, c + dc].reshape(8 * TOK, DIM)
-            s = halves(dot_nt(k, q))
-            pulls = halves(dot_nt(v, g))
-            weights, slopes = [], []
-            for f in range(2):
-                ws, ss = [], []
-                for df in range(3):
-                    tile = st[j, c + dc, f + df]
-                    level = jnp.where(in_grid(c, f, dc, df), tile[0:1], FAR)
-                    cut = slice(df * DIM, (df + 1) * DIM)
-                    w = jnp.exp2(s[f][:, cut] * SCALE - level)
-                    ws.append(w.astype(jnp.bfloat16))
-                    ss.append((w * (pulls[f][:, cut] - tile[1:2])).astype(jnp.bfloat16))
-                weights.append(jnp.concatenate(ws, axis=1))
-                slopes.append(jnp.concatenate(ss, axis=1))
-            grad_v += dot_nn(pair(*weights), g)
-            grad_k += dot_nn(pair(*slopes), q)
-        stage[2, j, c] = (grad_k * FACTOR).astype(jnp.bfloat16).reshape(2, 2, TOK, DIM)
-        stage[3, j, c] = grad_v.astype(jnp.bfloat16).reshape(2, 2, TOK, DIM)
-
-    def blocks(run, j):
+
+        def rows_of(ci, fi):
+            tile = st[j, ci, fi]
+            return jnp.where(in_grid(ci, fi), tile[0:1], FAR), tile[1:2]
+
+        def weigh(s, x, ci, fi):
+            level, dots = rows_of(ci, fi)
+            w = jnp.exp2(s * SCALE - level)
+            return w.astype(jnp.bfloat16), (w * (x - dots)).astype(jnp.bfloat16)
+
+        scores = against(k, qg, j, 0, c)
+        pulls = against(v, qg, j, 1, c)
+        near = [weigh(scores[n], pulls[n], c + n // 2, 1 + n % 2) for n in range(6)]
+        far = [
+            [weigh(scores[6 + n][own[f]], pulls[6 + n][own[f]], c + n, 3 * f) for n in range(3)]
+            for f in range(2)
+        ]
+        grads = []
+        for i, t in ((0, 1), (1, 0)):
+            left = jnp.concatenate([x[i] for x in near], axis=1)
+            right = by_rows(lambda f: jnp.concatenate([x[i] for x in far[f]], axis=1))
+            grads.append(times(left, right, qg, j, t, c))
+        stage[2, j, c] = (grads[1] * FACTOR).astype(jnp.bfloat16).reshape(2, 2, TOK, DIM)
+        stage[3, j, c] = grads[0].astype(jnp.bfloat16).reshape(2, 2, TOK, DIM)
+
+    def blocks(run, j, ts):
         def one(c, carry):
             run(j, c)
+            send_back(j, c, ts)
             return carry
 
         lax.fori_loop(0, 2, one, 0)
 
-    def send_back(j, ts):
+    def send_back(j, c, ts):
         for t in ts:
             for p in (1, 2, 0):
-                back_copy(p, t, j).start()
-            keep_copy(t, j).start()
+                back_copy(p, t, j, c).start()
+            keep_copy(t, j, c).start()
 
     def query_side(j):
         settle(z_recv.at[0, j], kv.at[j, :, pl.ds(1, 2), pl.ds(0, 2)])
         settle(cz_recv.at[j], kv.at[j, :, pl.ds(0, 2), pl.ds(0, 2)])
-        blocks(query_block, j)
+        blocks(query_block, j, (0, 1))
         for n in range(8):
             stat_copy(j, n).start()
-        send_back(j, (0, 1))
 
     def key_side(j):
         settle(y_recv.at[1, j], qg.at[j, :, pl.ds(0, 2), pl.ds(1, 2)])
         settle(cy_recv.at[j], qg.at[j, :, pl.ds(0, 2), pl.ds(0, 2)])
         settle(st_recv.at[j], st.at[j, pl.ds(0, 3)])
-        blocks(key_block, j)
-        send_back(j, (2, 3))
+        blocks(key_block, j, (2, 3))
 
     first_hops(0, 0)
     first_hops(1, 0)

time: 58.5 us -> 57 us (0.974)
  Pallas kernels: 57.7 us -> 56.2 us
    pallas_call x1, Pallas kernels: 56.6 us -> 55 us  [body(): pl.pallas_call(kernel, out_shape=[jax.ShapeDtypeStruct(queries.shape, jnp...]
where the time goes in v3:
time: 57 us; the launch traced here: 56.8 us
  Pallas kernels  56.2 us (99%)
  between operations  0.64 us (1%)
    pallas_call x1, Pallas kernels, body(): pl.pallas_call(kernel, out_shape=[jax.ShapeDtypeStruct(queries.shape, jnp...  55 us
    pallas_call x1, Pallas kernels, body(): pl.pallas_call(drain, out_shape=[jax.ShapeDtypeStruct(queries.shape, jnp....  1.17 us

profile of v3, /device:TPU:1, one launch (start us, length us, event | category | flops | bytes accessed | tf_op | source)
XLA Modules:
  0.0 56.8 jit_solution(12648444852854421597)
XLA Ops:
  0.6 55.0 %shard_map.75 = (bf16[1,1,2,64,1536]{4,3,2,1,0:T(8,128)(2,1)S(1)}, bf16[1,1,2,64,1536]{4,3,2,1,0:T(8,128)(2,1)S(1)}, bf16[1,1,2,64,1536]{4,3,2,1,0:T(8,128)(2,1)S(1)}, bf16[1,1,2,64,1536]{4,3,2,1,0:T(8,128)(2,1)S(1)}) custom-call(bf16[1,1,2,64,1536]{4,3,2,1,0:T(8,128)(2,1)} %q_in.1, bf16[1,1,2,64,1536]{4,3,2,1,0:T(8,128)(2,1)} %k_in.1, ...), custom_call_target="tpu_custom_call" | custom-call | tf_op jit(solution)/shard_map/pallas_call | solution.py:337
  55.7 1.2 %shard_map.76 = (bf16[1,1,2,64,1536]{4,3,2,1,0:T(8,128)(2,1)}, bf16[1,1,2,64,1536]{4,3,2,1,0:T(8,128)(2,1)}, bf16[1,1,2,64,1536]{4,3,2,1,0:T(8,128)(2,1)}, bf16[1,1,2,64,1536]{4,3,2,1,0:T(8,128)(2,1)}) custom-call(bf16[1,1,2,64,1536]{4,3,2,1,0:T(8,128)(2,1)S(1)} %get-tuple-element.8.refs_0_, bf16[1,1,2,64,1536]{4,3,2,1,0:T(8,128)(2,1)S(1)} %get-tuple-element.9.refs_1_, ...), custom_call_target="tpu_custom_call" | custom-call | tf_op jit(solution)/shard_map/pallas_call | solution.py:364
